TPU v7x, 256 devices: a whole 4x4x8 slice. The times are simulated.
256 devices in a mesh: row: 8 (over y, core), col: 32 (over x, z).
Axes of the slice: x: 4, y: 4, z: 8, core: 2. Of those that a mesh axis runs over, the one named last changes fastest.
Arguments:
- x_blocks: bfloat16 [8, 32, 42, 128, 128], P('row', 'col'), may hold values from -1.1953125 to 1.1953125
- x_slots: int32 [8, 32, 42], replicated, may hold values from 0 to 255, as said below
- x_count: int32 [8, 32], replicated, may hold values from 21 to 42, as said below
- s_slots: int32 [8, 32, 2], replicated, may hold values from 0 to 15, as said below
- s_count: int32 [8, 32], replicated, may hold values from 1 to 2, as said below
Outputs:
- square_blocks: bfloat16 [8, 32, 2, 128, 128], P('row', 'col')
- result_blocks: bfloat16 [8, 32, 2, 128, 128], P('row', 'col')
Inputs may be any that keep to these rules, and one draw needn't show every extreme that they name: `x_slots`: in each tile the live slots hold distinct positions; the live blocks whose position % 32 is below 2 come first among the live slots, at most 2 of them, and some tile has exactly 2. Positions of slots that are not live are arbitrary within the range. `x_count`: some tile has exactly 42 live slots. `s_slots`: in each tile the live slots hold distinct positions. `s_count`: some tile has exactly 2 live slots.
All inputs are finite; a program needn't handle non-finite values.
Results may differ from a plain program's by a relative error of at most 0.0049.
Values may be sent and summed in bfloat16 or wider, within the bound.
A program may use at most 128 MiB of HBM per device.

v0:
```python
import math
import jax
import jax.numpy as jnp
from jax import lax
from jax.sharding import PartitionSpec as P

RB = 8
JW = 2
CAPW = 2


def laid_out(pieces, dim):
    dims = list(pieces.shape[1:])
    dims[dim] *= pieces.shape[0]
    return jnp.moveaxis(pieces, 0, dim).reshape(dims)


def copy_for_each(array, axis):
    length = lax.axis_size(axis)
    return lax.all_to_all(
        jnp.broadcast_to(array[None], (length, *array.shape)), axis, 0, 0, tiled=True
    )


def gathered_copies(array, axis, dim):
    return laid_out(copy_for_each(array, axis), dim)


def match_index(targets, slot_keys, slot_live):
    matches = (targets[..., None] == slot_keys) & slot_live
    ordinal = jnp.arange(1, slot_keys.shape[0] + 1, dtype=jnp.int32)
    located = jnp.sum(jnp.where(matches, ordinal, 0), axis=-1)
    return jnp.where(located > 0, located - 1, slot_keys.shape[0])


def local(x_blocks, x_slots, x_count, s_slots, s_count):
    row_total = lax.axis_size("row")
    col_total = lax.axis_size("col")
    row_id = lax.axis_index("row")
    col_id = lax.axis_index("col")
    capacity = x_blocks.shape[2]
    block_size = x_blocks.shape[3]
    order_blocks = RB * col_total
    tile_width = order_blocks // row_total
    panel_all = lax.all_gather(x_blocks, "row", axis=0, tiled=True)
    stacked = panel_all.reshape(row_total * capacity, block_size, block_size)
    padded = jnp.concatenate(
        [stacked, jnp.zeros((1, block_size, block_size), stacked.dtype)], axis=0
    )
    column_slots = lax.dynamic_index_in_dim(x_slots, col_id, 1, keepdims=False)
    column_count = lax.dynamic_index_in_dim(x_count, col_id, 1, keepdims=False)
    ordinal = jnp.arange(capacity, dtype=jnp.int32)
    panel_live = (ordinal[None, :] < column_count[:, None]).reshape(-1)
    owners = jnp.arange(row_total, dtype=jnp.int32)[:, None]
    panel_keys = (
        column_slots // tile_width * order_blocks + owners * tile_width + column_slots % tile_width
    ).reshape(-1)
    row_lanes = jnp.arange(RB, dtype=jnp.int32)
    window_ids = jnp.arange(JW, dtype=jnp.int32)

    def accumulate(running, values, inner_row, inner_col, usable):
        picked = match_index(
            row_lanes[None, :] * order_blocks + inner_row[:, None], panel_keys, panel_live
        )
        left_part = jnp.take(padded, picked, axis=0)
        placing = ((inner_col[:, None] == window_ids[None, :]) & usable[:, None]).astype(
            values.dtype
        )
        placed = placing[:, :, None, None] * values[:, None, :, :]
        return running + jnp.einsum(
            "nrxy,njyz->rjxz", left_part, placed, preferred_element_type=jnp.float32
        )

    def make_step(slot_table, count_row, stride, column_limit):

        def fold_step(running, piece, offset):
            pieces = piece.shape[1]
            slot_count = piece.shape[2]
            positions = lax.dynamic_slice_in_dim(slot_table, offset, pieces, 0)[:, :slot_count]
            counts = lax.dynamic_slice_in_dim(count_row, offset, pieces, 0)
            owner_ids = offset + jnp.arange(pieces, dtype=jnp.int32)[:, None]
            inner_row = owner_ids * RB + positions // stride
            inner_col = positions % stride
            usable = (jnp.arange(slot_count, dtype=jnp.int32)[None, :] < counts[:, None]) & (
                inner_col < column_limit
            )
            values = piece.reshape(pieces * slot_count, block_size, block_size)
            return accumulate(
                running, values, inner_row.reshape(-1), inner_col.reshape(-1), usable.reshape(-1)
            )

        return fold_step

    blank_sum = jnp.zeros((RB, JW, block_size, block_size), jnp.float32)

    def collect_all(gathered, fold_step):
        per_turn = math.gcd(col_total, 8)

        def advance(turn_index, running):
            offset = turn_index * per_turn
            portion = lax.dynamic_slice_in_dim(gathered, offset, per_turn, 1)
            return fold_step(running, portion, offset)

        return lax.fori_loop(0, col_total // per_turn, advance, blank_sum)

    row_slots = lax.dynamic_index_in_dim(x_slots, row_id, 0, keepdims=False)
    row_count = lax.dynamic_index_in_dim(x_count, row_id, 0, keepdims=False)
    square_slots = lax.dynamic_index_in_dim(s_slots, row_id, 0, keepdims=False)
    square_count = lax.dynamic_index_in_dim(s_count, row_id, 0, keepdims=False)
    window_part = x_blocks[:, :, :CAPW]
    first_step = make_step(row_slots, row_count, tile_width, JW)
    product = collect_all(gathered_copies(window_part, "col", 1), first_step)
    own_slots = lax.dynamic_index_in_dim(square_slots, col_id, 0, keepdims=False)
    own_count = lax.dynamic_index_in_dim(square_count, col_id, 0, keepdims=False)
    own_live = jnp.arange(own_slots.shape[0], dtype=jnp.int32) < own_count
    flat_one = product.reshape(RB * JW, block_size, block_size)
    square_part = jnp.where(
        own_live[:, None, None], jnp.take(flat_one, own_slots, axis=0), 0.0
    ).astype(jnp.bfloat16)
    square_part = square_part[None, None]
    second_step = make_step(square_slots, square_count, JW, JW)
    second = collect_all(gathered_copies(square_part, "col", 1), second_step)
    own_keys = own_slots // JW * order_blocks + row_id * tile_width + own_slots % JW
    own_block = jnp.take(padded, match_index(own_keys, panel_keys, panel_live), axis=0).astype(
        jnp.float32
    )
    flat_two = second.reshape(RB * JW, block_size, block_size)
    combined = 1.5 * own_block - 0.5 * jnp.take(flat_two, own_slots, axis=0)
    result = jnp.where(own_live[:, None, None], combined, 0.0).astype(jnp.bfloat16)
    return (square_part, result[None, None])


def solution(mesh):
    in_specs = (P("row", "col", None, None, None), P(), P(), P(), P())
    out_specs = (P("row", "col", None, None, None), P("row", "col", None, None, None))
    return jax.shard_map(local, mesh=mesh, in_specs=in_specs, out_specs=out_specs, check_vma=False)
```

profile of v0, /device:TPU:1, one launch (start us, length us, event | category | flops | bytes accessed | tf_op | source)
XLA Modules:
  0.0 268.8 jit_solution(12169378988364675214)
XLA Ops:
  7.9 0.8 slice_bitcast_fusion
  8.9 1.9 broadcast_in_dim.199
  10.8 11.9 %all-to-all-start = ((bf16[32,1,1,2,128,128]{4,5,3,2,1,0:T(8,128)(2,1)}), bf16[32,1,1,2,128,128]{4,5,3,2,1,0:T(8,128)(2,1)S(1)}, u32[]{:S(2)}, u32[]{:S(2)}) async-start(bf16[32,1,1,2,128,128]{4,5,3,2,1,0:T(8,128)(2,1)} %broadcast_in_dim.199), calls=%async_computation | async-start | bytes 4194304 | tf_op jit(solution)/shard_map/all_to_all | solution.py:20
  23.2 1.4 fusion.74
  25.5 1.3 dynamic_slice.97
  28.4 48.9 %all-gather.2.cloned.1.call-done = bf16[8,1,42,128,128]{4,3,2,1,0:T(8,128)(2,1)} async-done(((bf16[1,1,42,128,128]{4,3,2,1,0:T(8,128)(2,1)}), bf16[8,1,42,128,128]{4,3,2,1,0:T(8,128)(2,1)}) %all-gather.2.cloned.1.call-update) | async-done | bytes 11010064 | tf_op jit(solution)/shard_map/all_gather | solution.py:45
  77.3 10.6 %concatenate.3 = bf16[337,128,128]{2,1,0:T(8,128)(2,1)} pad(bf16[336,128,128]{2,1,0:T(8,128)(2,1)} %bitcast.101, bf16[]{:T(256)} %constant.410.clone.1), padding=0_1x0_0x0_0 | pad | bytes 22052866 | tf_op jit(solution)/shard_map/concatenate | solution.py:47
  87.9 54.0 %while.36 = (s32[]{:T(128)}, f32[8,2,128,128]{2,3,0,1:T(8,128)}, s32[32,42]{1,0:T(8,128)S(1)}, s32[32]{0:T(128)S(1)}, bf16[1,32,2,128,128]{3,4,2,1,0:T(8,128)(2,...) while((s32[]{:T(128)}, f32[8,2,128,128]{2,3,0,1:T(8,128)}, ...), condition=%wide.wide.region_2.4_spmd.clone, body=%wide.wide.region_0.3_spmd.clone.sunk | while | flops 1078636672 | bytes 16272037 | solution.py:104
  89.0 7.3 %gather_fusion = bf16[128,128,128]{2,1,0:T(8,128)(2,1)} fusion(bf16[337,128,128]{2,1,0:T(8,128)(2,1)} %get-tuple-element.924, s32[1024]{0:T(1024)S(1)} %pad_clamp_fusion.8), kind=kCustom, calls=%fused_computation.clone.clone.clone.1 | custom fusion | bytes 8389120 | tf_op jit(solution)/shard_map/while/body/eval_jaxpr/jit(_take)/gather | solution.py:65
  96.6 4.6 %fusion.100 = f32[8,2,128,128]{2,3,0,1:T(8,128)} fusion(bf16[16,8,128,128]{3,2,1,0:T(8,128)(2,1)} %bitcast.97, pred[16,8]{0,1:T(8,128)(4,1)S(1)} %copy.73, f32[8,2,128,128]{2,3,0,1:T(8,128)} %get-tuple-element.906, bf16[16,128,128]{1,2,0:T(8,128)(2,1)S(1)} %bitcast.99, bf16[16,2]{0,1:T(2,128)(2,1)S(1)} %and_convert_fusion.6, pred[]{:T(512)S(6)} %compare.58), kind=kOutput, calls=%fused_computation.17.clone.clone.1 | convolution fusion | flops 1078460416 | bytes 6815937 | tf_op jit(solution)/shard_map/while/body/eval_jaxpr/nrxy,njyz->rjxz/dot_general | solution.py:70
  102.3 7.3 %gather_fusion = bf16[128,128,128]{2,1,0:T(8,128)(2,1)} fusion(bf16[337,128,128]{2,1,0:T(8,128)(2,1)} %get-tuple-element.924, s32[1024]{0:T(1024)S(1)} %pad_clamp_fusion.8), kind=kCustom, calls=%fused_computation.clone.clone.clone.1 | custom fusion | bytes 8389120 | tf_op jit(solution)/shard_map/while/body/eval_jaxpr/jit(_take)/gather | solution.py:65
  109.9 4.8 %fusion.100 = f32[8,2,128,128]{2,3,0,1:T(8,128)} fusion(bf16[16,8,128,128]{3,2,1,0:T(8,128)(2,1)} %bitcast.97, pred[16,8]{0,1:T(8,128)(4,1)S(1)} %copy.73, f32[8,2,128,128]{2,3,0,1:T(8,128)} %get-tuple-element.906, bf16[16,128,128]{1,2,0:T(8,128)(2,1)S(1)} %bitcast.99, bf16[16,2]{0,1:T(2,128)(2,1)S(1)} %and_convert_fusion.6, pred[]{:T(512)S(6)} %compare.58), kind=kOutput, calls=%fused_computation.17.clone.clone.1 | convolution fusion | flops 1078460416 | bytes 6815937 | tf_op jit(solution)/shard_map/while/body/eval_jaxpr/nrxy,njyz->rjxz/dot_general | solution.py:70
  115.9 7.3 %gather_fusion = bf16[128,128,128]{2,1,0:T(8,128)(2,1)} fusion(bf16[337,128,128]{2,1,0:T(8,128)(2,1)} %get-tuple-element.924, s32[1024]{0:T(1024)S(1)} %pad_clamp_fusion.8), kind=kCustom, calls=%fused_computation.clone.clone.clone.1 | custom fusion | bytes 8389120 | tf_op jit(solution)/shard_map/while/body/eval_jaxpr/jit(_take)/gather | solution.py:65
  123.5 4.8 %fusion.100 = f32[8,2,128,128]{2,3,0,1:T(8,128)} fusion(bf16[16,8,128,128]{3,2,1,0:T(8,128)(2,1)} %bitcast.97, pred[16,8]{0,1:T(8,128)(4,1)S(1)} %copy.73, f32[8,2,128,128]{2,3,0,1:T(8,128)} %get-tuple-element.906, bf16[16,128,128]{1,2,0:T(8,128)(2,1)S(1)} %bitcast.99, bf16[16,2]{0,1:T(2,128)(2,1)S(1)} %and_convert_fusion.6, pred[]{:T(512)S(6)} %compare.58), kind=kOutput, calls=%fused_computation.17.clone.clone.1 | convolution fusion | flops 1078460416 | bytes 6815937 | tf_op jit(solution)/shard_map/while/body/eval_jaxpr/nrxy,njyz->rjxz/dot_general | solution.py:70
  129.4 7.3 %gather_fusion = bf16[128,128,128]{2,1,0:T(8,128)(2,1)} fusion(bf16[337,128,128]{2,1,0:T(8,128)(2,1)} %get-tuple-element.924, s32[1024]{0:T(1024)S(1)} %pad_clamp_fusion.8), kind=kCustom, calls=%fused_computation.clone.clone.clone.1 | custom fusion | bytes 8389120 | tf_op jit(solution)/shard_map/while/body/eval_jaxpr/jit(_take)/gather | solution.py:65
  137.0 4.8 %fusion.100 = f32[8,2,128,128]{2,3,0,1:T(8,128)} fusion(bf16[16,8,128,128]{3,2,1,0:T(8,128)(2,1)} %bitcast.97, pred[16,8]{0,1:T(8,128)(4,1)S(1)} %copy.73, f32[8,2,128,128]{2,3,0,1:T(8,128)} %get-tuple-element.906, bf16[16,128,128]{1,2,0:T(8,128)(2,1)S(1)} %bitcast.99, bf16[16,2]{0,1:T(2,128)(2,1)S(1)} %and_convert_fusion.6, pred[]{:T(512)S(6)} %compare.58), kind=kOutput, calls=%fused_computation.17.clone.clone.1 | convolution fusion | flops 1078460416 | bytes 6815937 | tf_op jit(solution)/shard_map/while/body/eval_jaxpr/nrxy,njyz->rjxz/dot_general | solution.py:70
  141.9 1.5 copy.37
  144.2 1.9 broadcast_in_dim.207
  146.0 9.6 %all-to-all-start.1 = ((bf16[32,1,1,2,128,128]{4,5,3,2,1,0:T(8,128)(2,1)}), bf16[32,1,1,2,128,128]{4,5,3,2,1,0:T(8,128)(2,1)S(1)}, u32[]{:S(2)}, u32[]{:S(2)}) async-start(bf16[32,1,1,2,128,128]{4,5,3,2,1,0:T(8,128)(2,1)} %broadcast_in_dim.207), calls=%async_computation.1 | async-start | bytes 4194304 | tf_op jit(solution)/shard_map/all_to_all | solution.py:20
  156.4 4.7 %gather_fusion.2 = bf16[2,128,128]{2,1,0:T(8,128)(2,1)S(1)} fusion(bf16[337,128,128]{2,1,0:T(8,128)(2,1)} %get-tuple-element.971, s32[1024]{0:T(1024)S(1)} %pad_clamp_fusion.2), kind=kCustom, calls=%fused_computation.4 | custom fusion | bytes 131080 | tf_op jit(solution)/shard_map/jit(_take)/gather | solution.py:124
  161.8 42.7 %all-to-all-done.1 = bf16[32,1,1,2,128,128]{4,5,3,2,1,0:T(8,128)(2,1)S(1)} async-done(((bf16[32,1,1,2,128,128]{4,5,3,2,1,0:T(8,128)(2,1)}), bf16[32,1,1,2,128,128]{4,5,3,2,1,0:T(8,128)(2,1)S(1)}, u32[]{:S(2)}, u32[]{:S(2)}) %all-to-all-start.1) | async-done | bytes 2097184 | tf_op jit(solution)/shard_map/all_to_all | solution.py:20
  204.5 54.6 %while.37 = (s32[]{:T(128)}, f32[8,2,128,128]{2,3,0,1:T(8,128)}, s32[32,2]{0,1:T(2,128)S(1)}, s32[32]{0:T(128)S(1)}, bf16[1,32,2,128,128]{3,4,2,1,0:T(8,128)(2,1...) while((s32[]{:T(128)}, f32[8,2,128,128]{2,3,0,1:T(8,128)}, ...), condition=%wide.wide.region_6.9_spmd.clone, body=%wide.wide.region_4.8_spmd.clone.sunk | while | flops 1078636672 | bytes 16269573 | solution.py:104
  206.0 7.3 %gather_fusion.1 = bf16[128,128,128]{2,1,0:T(8,128)(2,1)} fusion(bf16[337,128,128]{2,1,0:T(8,128)(2,1)} %get-tuple-element.963, s32[1024]{0:T(1024)S(1)} %pad_clamp_fusion.9), kind=kCustom, calls=%fused_computation.2.clone.clone.clone.1 | custom fusion | bytes 8389120 | tf_op jit(solution)/shard_map/while/body/eval_jaxpr/jit(_take)/gather | solution.py:65
  213.4 4.6 %fusion.105 = f32[8,2,128,128]{2,3,0,1:T(8,128)} fusion(bf16[16,8,128,128]{3,2,1,0:T(8,128)(2,1)} %bitcast.98, pred[16,8]{0,1:T(8,128)(4,1)S(1)} %copy.76, f32[8,2,128,128]{2,3,0,1:T(8,128)} %get-tuple-element.945, bf16[16,128,128]{1,2,0:T(8,128)(2,1)S(1)} %bitcast.100, bf16[16,2]{0,1:T(2,128)(2,1)S(1)} %and_convert_fusion.7, pred[]{:T(512)S(6)} %compare.59), kind=kOutput, calls=%fused_computation.53.clone.clone.1 | convolution fusion | flops 1078460416 | bytes 6815937 | tf_op jit(solution)/shard_map/while/body/eval_jaxpr/nrxy,njyz->rjxz/dot_general | solution.py:70
  219.4 7.3 %gather_fusion.1 = bf16[128,128,128]{2,1,0:T(8,128)(2,1)} fusion(bf16[337,128,128]{2,1,0:T(8,128)(2,1)} %get-tuple-element.963, s32[1024]{0:T(1024)S(1)} %pad_clamp_fusion.9), kind=kCustom, calls=%fused_computation.2.clone.clone.clone.1 | custom fusion | bytes 8389120 | tf_op jit(solution)/shard_map/while/body/eval_jaxpr/jit(_take)/gather | solution.py:65
  226.8 4.8 %fusion.105 = f32[8,2,128,128]{2,3,0,1:T(8,128)} fusion(bf16[16,8,128,128]{3,2,1,0:T(8,128)(2,1)} %bitcast.98, pred[16,8]{0,1:T(8,128)(4,1)S(1)} %copy.76, f32[8,2,128,128]{2,3,0,1:T(8,128)} %get-tuple-element.945, bf16[16,128,128]{1,2,0:T(8,128)(2,1)S(1)} %bitcast.100, bf16[16,2]{0,1:T(2,128)(2,1)S(1)} %and_convert_fusion.7, pred[]{:T(512)S(6)} %compare.59), kind=kOutput, calls=%fused_computation.53.clone.clone.1 | convolution fusion | flops 1078460416 | bytes 6815937 | tf_op jit(solution)/shard_map/while/body/eval_jaxpr/nrxy,njyz->rjxz/dot_general | solution.py:70
  233.1 7.3 %gather_fusion.1 = bf16[128,128,128]{2,1,0:T(8,128)(2,1)} fusion(bf16[337,128,128]{2,1,0:T(8,128)(2,1)} %get-tuple-element.963, s32[1024]{0:T(1024)S(1)} %pad_clamp_fusion.9), kind=kCustom, calls=%fused_computation.2.clone.clone.clone.1 | custom fusion | bytes 8389120 | tf_op jit(solution)/shard_map/while/body/eval_jaxpr/jit(_take)/gather | solution.py:65
  240.5 4.8 %fusion.105 = f32[8,2,128,128]{2,3,0,1:T(8,128)} fusion(bf16[16,8,128,128]{3,2,1,0:T(8,128)(2,1)} %bitcast.98, pred[16,8]{0,1:T(8,128)(4,1)S(1)} %copy.76, f32[8,2,128,128]{2,3,0,1:T(8,128)} %get-tuple-element.945, bf16[16,128,128]{1,2,0:T(8,128)(2,1)S(1)} %bitcast.100, bf16[16,2]{0,1:T(2,128)(2,1)S(1)} %and_convert_fusion.7, pred[]{:T(512)S(6)} %compare.59), kind=kOutput, calls=%fused_computation.53.clone.clone.1 | convolution fusion | flops 1078460416 | bytes 6815937 | tf_op jit(solution)/shard_map/while/body/eval_jaxpr/nrxy,njyz->rjxz/dot_general | solution.py:70
  246.8 7.3 %gather_fusion.1 = bf16[128,128,128]{2,1,0:T(8,128)(2,1)} fusion(bf16[337,128,128]{2,1,0:T(8,128)(2,1)} %get-tuple-element.963, s32[1024]{0:T(1024)S(1)} %pad_clamp_fusion.9), kind=kCustom, calls=%fused_computation.2.clone.clone.clone.1 | custom fusion | bytes 8389120 | tf_op jit(solution)/shard_map/while/body/eval_jaxpr/jit(_take)/gather | solution.py:65
  254.2 4.8 %fusion.105 = f32[8,2,128,128]{2,3,0,1:T(8,128)} fusion(bf16[16,8,128,128]{3,2,1,0:T(8,128)(2,1)} %bitcast.98, pred[16,8]{0,1:T(8,128)(4,1)S(1)} %copy.76, f32[8,2,128,128]{2,3,0,1:T(8,128)} %get-tuple-element.945, bf16[16,128,128]{1,2,0:T(8,128)(2,1)S(1)} %bitcast.100, bf16[16,2]{0,1:T(2,128)(2,1)S(1)} %and_convert_fusion.7, pred[]{:T(512)S(6)} %compare.59), kind=kOutput, calls=%fused_computation.53.clone.clone.1 | convolution fusion | flops 1078460416 | bytes 6815937 | tf_op jit(solution)/shard_map/while/body/eval_jaxpr/nrxy,njyz->rjxz/dot_general | solution.py:70
  259.1 1.6 copy.40
  261.2 0.7 fusion.54
  (216 shorter events, 18.4 us)
Async XLA Ops:
  7.2 18.2 %copy-start = (s32[8,32,2]{1,2,0:T(2,128)S(1)}, s32[8,32,2]{1,2,0:T(2,128)}, u32[]{:S(2)}) copy-start(s32[8,32,2]{1,2,0:T(2,128)} %param.16) | copy-start | bytes 6148
  7.2 17.6 %copy-start.3 = (s32[8,32]{1,0:T(8,128)S(1)}, s32[8,32]{1,0:T(8,128)}, u32[]{:S(2)}) copy-start(s32[8,32]{1,0:T(8,128)} %param.15) | copy-start | bytes 3076
  7.2 70.1 %all-gather.2.cloned.1.call-start = ((), (), s32[]{:S(2)}) async-start(), calls=%async_computation.2 | async-start | bytes 12386304 | tf_op jit(solution)/shard_map/all_gather | solution.py:45
  10.8 77.2 %all-to-all-start = ((bf16[32,1,1,2,128,128]{4,5,3,2,1,0:T(8,128)(2,1)}), bf16[32,1,1,2,128,128]{4,5,3,2,1,0:T(8,128)(2,1)S(1)}, u32[]{:S(2)}, u32[]{:S(2)}) async-start(bf16[32,1,1,2,128,128]{4,5,3,2,1,0:T(8,128)(2,1)} %broadcast_in_dim.199), calls=%async_computation | async-start | bytes 4194304 | tf_op jit(solution)/shard_map/all_to_all | solution.py:20
  24.7 63.2 %copy-start.1 = (s32[8,42]{1,0:T(8,128)}, s32[8,42]{1,0:T(8,128)S(1)}, u32[]{:S(2)}) copy-start(s32[8,42]{1,0:T(8,128)S(1)} %fusion.57) | copy-start | bytes 4036
  141.9 13.7 %copy-start.2 = (s32[8,42]{1,0:T(8,128)S(1)}, s32[8,42]{1,0:T(8,128)}, u32[]{:S(2)}) copy-start(s32[8,42]{1,0:T(8,128)} %get-tuple-element.981) | copy-start | bytes 4036
  146.0 58.5 %all-to-all-start.1 = ((bf16[32,1,1,2,128,128]{4,5,3,2,1,0:T(8,128)(2,1)}), bf16[32,1,1,2,128,128]{4,5,3,2,1,0:T(8,128)(2,1)S(1)}, u32[]{:S(2)}, u32[]{:S(2)}) async-start(bf16[32,1,1,2,128,128]{4,5,3,2,1,0:T(8,128)(2,1)} %broadcast_in_dim.207), calls=%async_computation.1 | async-start | bytes 4194304 | tf_op jit(solution)/shard_map/all_to_all | solution.py:20
Sparse Core Ops, SparseCore 0:
  9.8 67.4 all-gather.1
where the time goes:
time: 270 us; the launch traced here: 269 us
  local copies, waits for them, and re-layouts  93.6 us (35%)
  waiting for transfers between devices  92.3 us (34%)
  matrix products  38.2 us (14%)
  starting transfers between devices  21.5 us (8%)
  between operations  14.2 us (5%)
  other arithmetic  8.6 us (3%)
    gather x8, local copies, waits for them, and re-layouts, accumulate(): left_part = jnp.take(padded, picked, axis=0)  58.1 us
    all_gather x1, waiting for transfers between devices, local(): panel_all = lax.all_gather(x_blocks, 'row', axis=0, tiled=True)  48.9 us
    all_to_all x2, waiting for transfers between devices, copy_for_each(): lax.all_to_all(jnp.broadcast_to(array[None], (length, *array.shape)), axi...  42.7 us
    dot_general x8, matrix products, accumulate(): jnp.einsum('nrxy,njyz->rjxz', left_part, placed, preferred_element_type=j...  38.2 us
    all_to_all x2, starting transfers between devices, copy_for_each(): lax.all_to_all(jnp.broadcast_to(array[None], (length, *array.shape)), axi...  21.4 us
    concatenate x1, local copies, waits for them, and re-layouts, local(): jnp.concatenate([stacked, jnp.zeros((1, block_size, block_size), stacked....  10.6 us
  transfers between devices with their start and end apart: 3, of which 2 were waited for; matrix products, arithmetic and copies ran while one was open for 9% of the time, Pallas kernels for 0%

commit v1 on v0

--- a/solution.py
+++ b/solution.py
@@ -42,7 +42,9 @@
     block_size = x_blocks.shape[3]
     order_blocks = RB * col_total
     tile_width = order_blocks // row_total
-    panel_all = lax.all_gather(x_blocks, "row", axis=0, tiled=True)
+    panel_all = jnp.concatenate(
+        lax.all_to_all(jnp.stack([x_blocks] * lax.axis_size("row")), "row", 0, 0), axis=0
+    )
     stacked = panel_all.reshape(row_total * capacity, block_size, block_size)
     padded = jnp.concatenate(
         [stacked, jnp.zeros((1, block_size, block_size), stacked.dtype)], axis=0

time: 270 us -> 372 us (1.38)
  waiting for transfers between devices: 92.3 us -> 195 us
  between operations: 14.2 us -> 0.79 us
  local copies, waits for them, and re-layouts: 93.6 us -> 102 us
    all_to_all x0 -> x1, waiting for transfers between devices: none -> 121 us  [local(): lax.all_to_all(jnp.stack([x_blocks] * lax.axis_size('row')), 'row', 0, 0)]
    all_gather x1 -> x0, waiting for transfers between devices: 48.9 us -> none  [local(): panel_all = lax.all_gather(x_blocks, 'row', axis=0, tiled=True)]
    all_to_all x2, waiting for transfers between devices: 42.7 us -> 74.6 us  [copy_for_each(): lax.all_to_all(jnp.broadcast_to(array[None], (length, *array.shape)), axi...]
    another operation x0 -> x1, local copies, waits for them, and re-layouts: none -> 8.33 us  [local(): jnp.stack([x_blocks] * lax.axis_size('row'))]
    all_to_all x0 -> x1, starting transfers between devices: none -> 8.26 us  [local(): lax.all_to_all(jnp.stack([x_blocks] * lax.axis_size('row')), 'row', 0, 0)]
    all_to_all x2, starting transfers between devices: 21.4 us -> 16.4 us  [copy_for_each(): lax.all_to_all(jnp.broadcast_to(array[None], (length, *array.shape)), axi...]
  transfers between devices with their start and end apart: 3 -> 3, of which waited for: 2 -> 3; matrix products, arithmetic and copies ran while one was open for 9% -> 6% of each run, Pallas kernels for 0% -> 0%
where the time goes in v1:
time: 372 us; the launch traced here: 370 us
  waiting for transfers between devices  195 us (52%)
  local copies, waits for them, and re-layouts  102 us (27%)
  matrix products  38.2 us (10%)
  starting transfers between devices  24.7 us (7%)
  other arithmetic  8.73 us (2%)
    all_to_all x1, waiting for transfers between devices, local(): lax.all_to_all(jnp.stack([x_blocks] * lax.axis_size('row')), 'row', 0, 0)  121 us
    all_to_all x2, waiting for transfers between devices, copy_for_each(): lax.all_to_all(jnp.broadcast_to(array[None], (length, *array.shape)), axi...  74.6 us
    gather x8, local copies, waits for them, and re-layouts, accumulate(): left_part = jnp.take(padded, picked, axis=0)  58 us
    dot_general x8, matrix products, accumulate(): jnp.einsum('nrxy,njyz->rjxz', left_part, placed, preferred_element_type=j...  38.2 us
    all_to_all x2, starting transfers between devices, copy_for_each(): lax.all_to_all(jnp.broadcast_to(array[None], (length, *array.shape)), axi...  16.4 us
    concatenate x1, local copies, waits for them, and re-layouts, local(): jnp.concatenate([stacked, jnp.zeros((1, block_size, block_size), stacked....  10.6 us
    another operation x1, local copies, waits for them, and re-layouts, local(): jnp.stack([x_blocks] * lax.axis_size('row'))  8.33 us
    all_to_all x1, starting transfers between devices, local(): lax.all_to_all(jnp.stack([x_blocks] * lax.axis_size('row')), 'row', 0, 0)  8.26 us
  transfers between devices with their start and end apart: 3, of which 3 were waited for; matrix products, arithmetic and copies ran while one was open for 6% of the time, Pallas kernels for 0%

profile of v1, /device:TPU:1, one launch (start us, length us, event | category | flops | bytes accessed | tf_op | source)
XLA Modules:
  0.0 370.3 jit_solution(8045077735970027891)
XLA Ops:
  0.6 8.3 %stack.2 = bf16[8,1,1,42,128,128]{5,4,3,2,1,0:T(8,128)(2,1)} broadcast(bf16[42,128,128]{2,1,0:T(8,128)(2,1)} %bitcast.104), dimensions={3,4,5} | broadcast | bytes 12386304 | tf_op jit(solution)/shard_map/stack | solution.py:46
  9.0 8.3 %all-to-all-start.1 = ((bf16[8,1,1,42,128,128]{5,4,3,2,1,0:T(8,128)(2,1)}), bf16[8,1,1,42,128,128]{5,4,3,2,1,0:T(8,128)(2,1)}, u32[]{:S(2)}, u32[]{:S(2)}) async-start(bf16[8,1,1,42,128,128]{5,4,3,2,1,0:T(8,128)(2,1)} %stack.2), calls=%async_computation.1 | async-start | bytes 22020096 | tf_op jit(solution)/shard_map/all_to_all | solution.py:46
  18.2 120.9 %all-to-all-done.1 = bf16[8,1,1,42,128,128]{5,4,3,2,1,0:T(8,128)(2,1)} async-done(((bf16[8,1,1,42,128,128]{5,4,3,2,1,0:T(8,128)(2,1)}), bf16[8,1,1,42,128,128]{5,4,3,2,1,0:T(8,128)(2,1)}, u32[]{:S(2)}, u32[]{:S(2)}) %all-to-all-start.1) | async-done | bytes 11010080 | tf_op jit(solution)/shard_map/all_to_all | solution.py:46
  139.1 1.9 broadcast_in_dim.199
  140.9 9.3 %all-to-all-start = ((bf16[32,1,1,2,128,128]{4,5,3,2,1,0:T(8,128)(2,1)}), bf16[32,1,1,2,128,128]{4,5,3,2,1,0:T(8,128)(2,1)S(1)}, u32[]{:S(2)}, u32[]{:S(2)}) async-start(bf16[32,1,1,2,128,128]{4,5,3,2,1,0:T(8,128)(2,1)} %broadcast_in_dim.199), calls=%async_computation | async-start | bytes 4194304 | tf_op jit(solution)/shard_map/all_to_all | solution.py:20
  150.8 1.4 fusion.74
  156.2 10.6 %concatenate.3 = bf16[337,128,128]{2,1,0:T(8,128)(2,1)} pad(bf16[336,128,128]{2,1,0:T(8,128)(2,1)} %bitcast.7, bf16[]{:T(256)} %constant.410.clone.1), padding=0_1x0_0x0_0 | pad | bytes 22052866 | tf_op jit(solution)/shard_map/concatenate | solution.py:49
  166.8 32.1 %all-to-all-done = bf16[32,1,1,2,128,128]{4,5,3,2,1,0:T(8,128)(2,1)S(1)} async-done(((bf16[32,1,1,2,128,128]{4,5,3,2,1,0:T(8,128)(2,1)}), bf16[32,1,1,2,128,128]{4,5,3,2,1,0:T(8,128)(2,1)S(1)}, u32[]{:S(2)}, u32[]{:S(2)}) %all-to-all-start) | async-done | bytes 2097184 | tf_op jit(solution)/shard_map/all_to_all | solution.py:20
  199.0 53.9 %while.36 = (s32[]{:T(128)}, f32[8,2,128,128]{2,3,0,1:T(8,128)}, s32[32,42]{1,0:T(8,128)S(1)}, s32[32]{0:T(128)S(1)}, bf16[1,32,2,128,128]{3,4,2,1,0:T(8,128)(2,...) while((s32[]{:T(128)}, f32[8,2,128,128]{2,3,0,1:T(8,128)}, ...), condition=%wide.wide.region_2.4_spmd.clone, body=%wide.wide.region_0.3_spmd.clone.sunk | while | flops 1078636672 | bytes 16272037 | solution.py:106
  200.1 7.3 %gather_fusion = bf16[128,128,128]{2,1,0:T(8,128)(2,1)} fusion(bf16[337,128,128]{2,1,0:T(8,128)(2,1)} %get-tuple-element.924, s32[1024]{0:T(1024)S(1)} %pad_clamp_fusion.8), kind=kCustom, calls=%fused_computation.clone.clone.clone.1 | custom fusion | bytes 8389120 | tf_op jit(solution)/shard_map/while/body/eval_jaxpr/jit(_take)/gather | solution.py:67
  207.7 4.6 %fusion.100 = f32[8,2,128,128]{2,3,0,1:T(8,128)} fusion(bf16[16,8,128,128]{3,2,1,0:T(8,128)(2,1)} %bitcast.98, pred[16,8]{0,1:T(8,128)(4,1)S(1)} %copy.73, f32[8,2,128,128]{2,3,0,1:T(8,128)} %get-tuple-element.906, bf16[16,128,128]{1,2,0:T(8,128)(2,1)S(1)} %bitcast.100, bf16[16,2]{0,1:T(2,128)(2,1)S(1)} %and_convert_fusion.6, pred[]{:T(512)S(6)} %compare.58), kind=kOutput, calls=%fused_computation.17.clone.clone.1 | convolution fusion | flops 1078460416 | bytes 6815937 | tf_op jit(solution)/shard_map/while/body/eval_jaxpr/nrxy,njyz->rjxz/dot_general | solution.py:72
  213.3 7.3 %gather_fusion = bf16[128,128,128]{2,1,0:T(8,128)(2,1)} fusion(bf16[337,128,128]{2,1,0:T(8,128)(2,1)} %get-tuple-element.924, s32[1024]{0:T(1024)S(1)} %pad_clamp_fusion.8), kind=kCustom, calls=%fused_computation.clone.clone.clone.1 | custom fusion | bytes 8389120 | tf_op jit(solution)/shard_map/while/body/eval_jaxpr/jit(_take)/gather | solution.py:67
  220.9 4.8 %fusion.100 = f32[8,2,128,128]{2,3,0,1:T(8,128)} fusion(bf16[16,8,128,128]{3,2,1,0:T(8,128)(2,1)} %bitcast.98, pred[16,8]{0,1:T(8,128)(4,1)S(1)} %copy.73, f32[8,2,128,128]{2,3,0,1:T(8,128)} %get-tuple-element.906, bf16[16,128,128]{1,2,0:T(8,128)(2,1)S(1)} %bitcast.100, bf16[16,2]{0,1:T(2,128)(2,1)S(1)} %and_convert_fusion.6, pred[]{:T(512)S(6)} %compare.58), kind=kOutput, calls=%fused_computation.17.clone.clone.1 | convolution fusion | flops 1078460416 | bytes 6815937 | tf_op jit(solution)/shard_map/while/body/eval_jaxpr/nrxy,njyz->rjxz/dot_general | solution.py:72
  226.9 7.3 %gather_fusion = bf16[128,128,128]{2,1,0:T(8,128)(2,1)} fusion(bf16[337,128,128]{2,1,0:T(8,128)(2,1)} %get-tuple-element.924, s32[1024]{0:T(1024)S(1)} %pad_clamp_fusion.8), kind=kCustom, calls=%fused_computation.clone.clone.clone.1 | custom fusion | bytes 8389120 | tf_op jit(solution)/shard_map/while/body/eval_jaxpr/jit(_take)/gather | solution.py:67
  234.5 4.8 %fusion.100 = f32[8,2,128,128]{2,3,0,1:T(8,128)} fusion(bf16[16,8,128,128]{3,2,1,0:T(8,128)(2,1)} %bitcast.98, pred[16,8]{0,1:T(8,128)(4,1)S(1)} %copy.73, f32[8,2,128,128]{2,3,0,1:T(8,128)} %get-tuple-element.906, bf16[16,128,128]{1,2,0:T(8,128)(2,1)S(1)} %bitcast.100, bf16[16,2]{0,1:T(2,128)(2,1)S(1)} %and_convert_fusion.6, pred[]{:T(512)S(6)} %compare.58), kind=kOutput, calls=%fused_computation.17.clone.clone.1 | convolution fusion | flops 1078460416 | bytes 6815937 | tf_op jit(solution)/shard_map/while/body/eval_jaxpr/nrxy,njyz->rjxz/dot_general | solution.py:72
  240.4 7.3 %gather_fusion = bf16[128,128,128]{2,1,0:T(8,128)(2,1)} fusion(bf16[337,128,128]{2,1,0:T(8,128)(2,1)} %get-tuple-element.924, s32[1024]{0:T(1024)S(1)} %pad_clamp_fusion.8), kind=kCustom, calls=%fused_computation.clone.clone.clone.1 | custom fusion | bytes 8389120 | tf_op jit(solution)/shard_map/while/body/eval_jaxpr/jit(_take)/gather | solution.py:67
  248.0 4.8 %fusion.100 = f32[8,2,128,128]{2,3,0,1:T(8,128)} fusion(bf16[16,8,128,128]{3,2,1,0:T(8,128)(2,1)} %bitcast.98, pred[16,8]{0,1:T(8,128)(4,1)S(1)} %copy.73, f32[8,2,128,128]{2,3,0,1:T(8,128)} %get-tuple-element.906, bf16[16,128,128]{1,2,0:T(8,128)(2,1)S(1)} %bitcast.100, bf16[16,2]{0,1:T(2,128)(2,1)S(1)} %and_convert_fusion.6, pred[]{:T(512)S(6)} %compare.58), kind=kOutput, calls=%fused_computation.17.clone.clone.1 | convolution fusion | flops 1078460416 | bytes 6815937 | tf_op jit(solution)/shard_map/while/body/eval_jaxpr/nrxy,njyz->rjxz/dot_general | solution.py:72
  252.8 1.5 copy.37
  255.1 1.9 broadcast_in_dim.207
  257.0 7.1 %all-to-all-start.2 = ((bf16[32,1,1,2,128,128]{4,5,3,2,1,0:T(8,128)(2,1)}), bf16[32,1,1,2,128,128]{4,5,3,2,1,0:T(8,128)(2,1)S(1)}, u32[]{:S(2)}, u32[]{:S(2)}) async-start(bf16[32,1,1,2,128,128]{4,5,3,2,1,0:T(8,128)(2,1)} %broadcast_in_dim.207), calls=%async_computation.2 | async-start | bytes 4194304 | tf_op jit(solution)/shard_map/all_to_all | solution.py:20
  264.9 4.7 %gather_fusion.2 = bf16[2,128,128]{2,1,0:T(8,128)(2,1)S(1)} fusion(bf16[337,128,128]{2,1,0:T(8,128)(2,1)} %get-tuple-element.970, s32[1024]{0:T(1024)S(1)} %pad_clamp_fusion.2), kind=kCustom, calls=%fused_computation.4 | custom fusion | bytes 131080 | tf_op jit(solution)/shard_map/jit(_take)/gather | solution.py:126
  270.4 42.5 %all-to-all-done.2 = bf16[32,1,1,2,128,128]{4,5,3,2,1,0:T(8,128)(2,1)S(1)} async-done(((bf16[32,1,1,2,128,128]{4,5,3,2,1,0:T(8,128)(2,1)}), bf16[32,1,1,2,128,128]{4,5,3,2,1,0:T(8,128)(2,1)S(1)}, u32[]{:S(2)}, u32[]{:S(2)}) %all-to-all-start.2) | async-done | bytes 2097184 | tf_op jit(solution)/shard_map/all_to_all | solution.py:20
  312.8 54.6 %while.37 = (s32[]{:T(128)}, f32[8,2,128,128]{2,3,0,1:T(8,128)}, s32[32,2]{0,1:T(2,128)S(1)}, s32[32]{0:T(128)S(1)}, bf16[1,32,2,128,128]{3,4,2,1,0:T(8,128)(2,1...) while((s32[]{:T(128)}, f32[8,2,128,128]{2,3,0,1:T(8,128)}, ...), condition=%wide.wide.region_6.9_spmd.clone, body=%wide.wide.region_4.8_spmd.clone.sunk | while | flops 1078636672 | bytes 16269573 | solution.py:106
  314.3 7.3 %gather_fusion.1 = bf16[128,128,128]{2,1,0:T(8,128)(2,1)} fusion(bf16[337,128,128]{2,1,0:T(8,128)(2,1)} %get-tuple-element.963, s32[1024]{0:T(1024)S(1)} %pad_clamp_fusion.9), kind=kCustom, calls=%fused_computation.2.clone.clone.clone.1 | custom fusion | bytes 8389120 | tf_op jit(solution)/shard_map/while/body/eval_jaxpr/jit(_take)/gather | solution.py:67
  321.7 4.6 %fusion.105 = f32[8,2,128,128]{2,3,0,1:T(8,128)} fusion(bf16[16,8,128,128]{3,2,1,0:T(8,128)(2,1)} %bitcast.99, pred[16,8]{0,1:T(8,128)(4,1)S(1)} %copy.76, f32[8,2,128,128]{2,3,0,1:T(8,128)} %get-tuple-element.945, bf16[16,128,128]{1,2,0:T(8,128)(2,1)S(1)} %bitcast.101, bf16[16,2]{0,1:T(2,128)(2,1)S(1)} %and_convert_fusion.7, pred[]{:T(512)S(6)} %compare.59), kind=kOutput, calls=%fused_computation.53.clone.clone.1 | convolution fusion | flops 1078460416 | bytes 6815937 | tf_op jit(solution)/shard_map/while/body/eval_jaxpr/nrxy,njyz->rjxz/dot_general | solution.py:72
  327.7 7.3 %gather_fusion.1 = bf16[128,128,128]{2,1,0:T(8,128)(2,1)} fusion(bf16[337,128,128]{2,1,0:T(8,128)(2,1)} %get-tuple-element.963, s32[1024]{0:T(1024)S(1)} %pad_clamp_fusion.9), kind=kCustom, calls=%fused_computation.2.clone.clone.clone.1 | custom fusion | bytes 8389120 | tf_op jit(solution)/shard_map/while/body/eval_jaxpr/jit(_take)/gather | solution.py:67
  335.1 4.9 %fusion.105 = f32[8,2,128,128]{2,3,0,1:T(8,128)} fusion(bf16[16,8,128,128]{3,2,1,0:T(8,128)(2,1)} %bitcast.99, pred[16,8]{0,1:T(8,128)(4,1)S(1)} %copy.76, f32[8,2,128,128]{2,3,0,1:T(8,128)} %get-tuple-element.945, bf16[16,128,128]{1,2,0:T(8,128)(2,1)S(1)} %bitcast.101, bf16[16,2]{0,1:T(2,128)(2,1)S(1)} %and_convert_fusion.7, pred[]{:T(512)S(6)} %compare.59), kind=kOutput, calls=%fused_computation.53.clone.clone.1 | convolution fusion | flops 1078460416 | bytes 6815937 | tf_op jit(solution)/shard_map/while/body/eval_jaxpr/nrxy,njyz->rjxz/dot_general | solution.py:72
  341.4 7.3 %gather_fusion.1 = bf16[128,128,128]{2,1,0:T(8,128)(2,1)} fusion(bf16[337,128,128]{2,1,0:T(8,128)(2,1)} %get-tuple-element.963, s32[1024]{0:T(1024)S(1)} %pad_clamp_fusion.9), kind=kCustom, calls=%fused_computation.2.clone.clone.clone.1 | custom fusion | bytes 8389120 | tf_op jit(solution)/shard_map/while/body/eval_jaxpr/jit(_take)/gather | solution.py:67
  348.8 4.9 %fusion.105 = f32[8,2,128,128]{2,3,0,1:T(8,128)} fusion(bf16[16,8,128,128]{3,2,1,0:T(8,128)(2,1)} %bitcast.99, pred[16,8]{0,1:T(8,128)(4,1)S(1)} %copy.76, f32[8,2,128,128]{2,3,0,1:T(8,128)} %get-tuple-element.945, bf16[16,128,128]{1,2,0:T(8,128)(2,1)S(1)} %bitcast.101, bf16[16,2]{0,1:T(2,128)(2,1)S(1)} %and_convert_fusion.7, pred[]{:T(512)S(6)} %compare.59), kind=kOutput, calls=%fused_computation.53.clone.clone.1 | convolution fusion | flops 1078460416 | bytes 6815937 | tf_op jit(solution)/shard_map/while/body/eval_jaxpr/nrxy,njyz->rjxz/dot_general | solution.py:72
  355.1 7.3 %gather_fusion.1 = bf16[128,128,128]{2,1,0:T(8,128)(2,1)} fusion(bf16[337,128,128]{2,1,0:T(8,128)(2,1)} %get-tuple-element.963, s32[1024]{0:T(1024)S(1)} %pad_clamp_fusion.9), kind=kCustom, calls=%fused_computation.2.clone.clone.clone.1 | custom fusion | bytes 8389120 | tf_op jit(solution)/shard_map/while/body/eval_jaxpr/jit(_take)/gather | solution.py:67
  362.5 4.9 %fusion.105 = f32[8,2,128,128]{2,3,0,1:T(8,128)} fusion(bf16[16,8,128,128]{3,2,1,0:T(8,128)(2,1)} %bitcast.99, pred[16,8]{0,1:T(8,128)(4,1)S(1)} %copy.76, f32[8,2,128,128]{2,3,0,1:T(8,128)} %get-tuple-element.945, bf16[16,128,128]{1,2,0:T(8,128)(2,1)S(1)} %bitcast.101, bf16[16,2]{0,1:T(2,128)(2,1)S(1)} %and_convert_fusion.7, pred[]{:T(512)S(6)} %compare.59), kind=kOutput, calls=%fused_computation.53.clone.clone.1 | convolution fusion | flops 1078460416 | bytes 6815937 | tf_op jit(solution)/shard_map/while/body/eval_jaxpr/nrxy,njyz->rjxz/dot_general | solution.py:72
  367.4 1.6 copy.40
  (216 shorter events, 20.7 us)
Async XLA Ops:
  0.6 152.4 %copy-start = (s32[8,32,2]{1,2,0:T(2,128)S(1)}, s32[8,32,2]{1,2,0:T(2,128)}, u32[]{:S(2)}) copy-start(s32[8,32,2]{1,2,0:T(2,128)} %param.16) | copy-start | bytes 6148
  9.0 130.1 %all-to-all-start.1 = ((bf16[8,1,1,42,128,128]{5,4,3,2,1,0:T(8,128)(2,1)}), bf16[8,1,1,42,128,128]{5,4,3,2,1,0:T(8,128)(2,1)}, u32[]{:S(2)}, u32[]{:S(2)}) async-start(bf16[8,1,1,42,128,128]{5,4,3,2,1,0:T(8,128)(2,1)} %stack.2), calls=%async_computation.1 | async-start | bytes 22020096 | tf_op jit(solution)/shard_map/all_to_all | solution.py:46
  17.2 135.2 %copy-start.3 = (s32[8,32]{1,0:T(8,128)S(1)}, s32[8,32]{1,0:T(8,128)}, u32[]{:S(2)}) copy-start(s32[8,32]{1,0:T(8,128)} %param.15) | copy-start | bytes 3076
  140.9 58.0 %all-to-all-start = ((bf16[32,1,1,2,128,128]{4,5,3,2,1,0:T(8,128)(2,1)}), bf16[32,1,1,2,128,128]{4,5,3,2,1,0:T(8,128)(2,1)S(1)}, u32[]{:S(2)}, u32[]{:S(2)}) async-start(bf16[32,1,1,2,128,128]{4,5,3,2,1,0:T(8,128)(2,1)} %broadcast_in_dim.199), calls=%async_computation | async-start | bytes 4194304 | tf_op jit(solution)/shard_map/all_to_all | solution.py:20
  152.3 14.5 %copy-start.1 = (s32[8,42]{1,0:T(8,128)}, s32[8,42]{1,0:T(8,128)S(1)}, u32[]{:S(2)}) copy-start(s32[8,42]{1,0:T(8,128)S(1)} %fusion.57) | copy-start | bytes 4036
  252.8 11.3 %copy-start.2 = (s32[8,42]{1,0:T(8,128)S(1)}, s32[8,42]{1,0:T(8,128)}, u32[]{:S(2)}) copy-start(s32[8,42]{1,0:T(8,128)} %get-tuple-element.979) | copy-start | bytes 4036
  257.0 55.8 %all-to-all-start.2 = ((bf16[32,1,1,2,128,128]{4,5,3,2,1,0:T(8,128)(2,1)}), bf16[32,1,1,2,128,128]{4,5,3,2,1,0:T(8,128)(2,1)S(1)}, u32[]{:S(2)}, u32[]{:S(2)}) async-start(bf16[32,1,1,2,128,128]{4,5,3,2,1,0:T(8,128)(2,1)} %broadcast_in_dim.207), calls=%async_computation.2 | async-start | bytes 4194304 | tf_op jit(solution)/shard_map/all_to_all | solution.py:20
